TPU v7x, 32 devices: a whole 2x2x4 slice. The times are simulated.
32 devices in a mesh: beam: 4 (over y, x), row: 4 (over z), col: 2 (over core).
Axes of the slice: x: 2, y: 2, z: 4, core: 2. Of those that a mesh axis runs over, the one named last changes fastest.
Arguments:
- phase_volume: bfloat16 [64, 1024, 256], P('beam', 'row', 'col'), may hold values from -0.75 to 0.75
- absorb_volume: bfloat16 [64, 1024, 256], P('beam', 'row', 'col'), may hold values from -0.375 to 0.375
- probe: float32 [2, 256, 256], replicated, may hold values from -6 to 6
- amplitudes: bfloat16 [4, 2, 32, 256, 256], P('row', 'col', 'beam'), may hold values from 0.19921875 to 2.5
- scan_rows: int32 [4, 2, 32], P('row', 'col', 'beam'), may hold values from 0 to 255
- scan_cols: int32 [4, 2, 32], P('row', 'col', 'beam'), may hold values from 0 to 127
Outputs:
- object_step: float32 [2, 1024, 256], P(None, 'row', 'col')
- probe_gradient: float32 [2, 256, 256], replicated
- loss: float32 [], replicated
All inputs are finite; a program needn't handle non-finite values.
Results may differ from a plain program's by a relative error of at most 0.00055.
The roundings to bfloat16 on the way count: a program that leaves them out, or rounds other values in their place, can miss the bound.
Values sent between devices are 32-bit elements; how exact they have to be, the bound alone decides.
No kernel may reach another device: no remote copies, remote signals or barrier semaphores. Data moves between devices by JAX's collectives and lax.ppermute only.
A program may use at most 64 MiB of HBM per device.

v0:
```python
import math

import jax
import jax.numpy as jnp
from jax import lax
from jax.sharding import PartitionSpec as P


def from_behind(value, axis, steps):
    count = lax.axis_size(axis)
    first, last = (max(0, -steps), min(count, count - steps))
    return lax.ppermute(value, axis, [(source, source + steps) for source in range(first, last)])


def extended(cells, sides, width):
    for axis, dim in sides:
        count = lax.axis_size(axis)
        ends = count - 1
        head = lax.slice_in_dim(cells, 0, width, axis=dim)
        tail = lax.slice_in_dim(cells, cells.shape[dim] - width, cells.shape[dim], axis=dim)
        cells = jnp.concatenate(
            [
                lax.ppermute(tail, axis, [(i, (i + 1) % count) for i in range(ends)]),
                cells,
                lax.ppermute(head, axis, [((i + 1) % count, i) for i in range(ends)]),
            ],
            axis=dim,
        )
    return cells


def dft_tables(length):
    indices = jnp.arange(length, dtype=jnp.int32)
    product = indices[:, None] * indices[None, :] % length
    angles = product.astype(jnp.float32) * (2.0 * math.pi / length)
    factor = 1.0 / math.sqrt(length)
    return (
        (jnp.cos(angles) * factor).astype(jnp.bfloat16),
        (-jnp.sin(angles) * factor).astype(jnp.bfloat16),
    )


def fold_rims(canvas, half):
    rows_inner = canvas.shape[1] - 2 * half
    cols_inner = canvas.shape[2] - 2 * half
    middle = canvas[:, :, half : half + cols_inner]
    from_right = from_behind(canvas[:, :, :half], "col", -1)
    from_left = from_behind(canvas[:, :, half + cols_inner :], "col", 1)
    middle = middle + from_right
    middle = middle + from_left
    center = middle[:, half : half + rows_inner, :]
    from_below = from_behind(middle[:, :half, :], "row", -1)
    from_above = from_behind(middle[:, half + rows_inner :, :], "row", 1)
    center = center + jnp.pad(from_below, ((0, 0), (rows_inner - half, 0), (0, 0)))
    return center + jnp.pad(from_above, ((0, 0), (0, rows_inner - half), (0, 0)))


def local(phase_volume, absorb_volume, probe, amplitudes, scan_rows, scan_cols):
    length = probe.shape[1]
    half = length // 2
    count = scan_rows.shape[2]
    rows_local = phase_volume.shape[1]
    cols_local = phase_volume.shape[2]
    phase_part = jnp.sum(phase_volume, axis=0, dtype=jnp.float32)
    absorb_part = jnp.sum(absorb_volume, axis=0, dtype=jnp.float32)
    phase_sum, absorb_sum = lax.psum((phase_part, absorb_part), "beam")
    padded = extended(jnp.stack([phase_sum, absorb_sum]), (("row", 1), ("col", 2)), half)
    row_begin = scan_rows.reshape(count)
    col_begin = scan_cols.reshape(count)
    zero_index = jnp.zeros((), jnp.int32)
    windows = jax.vmap(
        lambda row_at, col_at: lax.dynamic_slice(
            padded, (zero_index, row_at, col_at), (2, length, length)
        )
    )(row_begin, col_begin)
    table_real, table_imag = dft_tables(length)
    negated = -table_imag
    forward_left = jnp.stack(
        [jnp.stack([table_real, negated]), jnp.stack([table_imag, table_real])]
    )
    forward_right = jnp.stack(
        [
            jnp.concatenate([table_real, table_imag], axis=1),
            jnp.concatenate([negated, table_real], axis=1),
        ]
    )
    backward_left = jnp.stack(
        [jnp.stack([table_real, table_imag]), jnp.stack([negated, table_real])]
    )
    backward_right = jnp.stack(
        [
            jnp.concatenate([table_real, negated], axis=1),
            jnp.concatenate([table_imag, table_real], axis=1),
        ]
    )
    damping = jnp.exp(-windows[:, 1])
    trans_real = damping * jnp.cos(windows[:, 0])
    trans_imag = damping * jnp.sin(windows[:, 0])
    wave_real = probe[0] * trans_real - probe[1] * trans_imag
    wave_imag = probe[0] * trans_imag + probe[1] * trans_real
    outgoing = jnp.stack([wave_real, wave_imag], axis=1).astype(jnp.bfloat16)
    half_wave = jnp.einsum(
        "yxab,sxbc->syac", forward_left, outgoing, preferred_element_type=jnp.float32
    ).astype(jnp.bfloat16)
    far_field = jnp.einsum(
        "sxab,xbd->sad", half_wave, forward_right, preferred_element_type=jnp.float32
    )
    far_real = far_field[:, :, :length]
    far_imag = far_field[:, :, length:]
    amplitude = amplitudes.reshape(count, length, length).astype(jnp.float32)
    modulus = jnp.sqrt(far_real * far_real + far_imag * far_imag)
    misfit = jnp.sum((modulus - amplitude) * (modulus - amplitude))
    ratio = 1.0 - amplitude / jnp.maximum(modulus, 0.5)
    residual = (far_field * jnp.concatenate([ratio, ratio], axis=2)).astype(jnp.bfloat16)
    back_half = jnp.einsum(
        "yxab,sbxc->syac",
        backward_left,
        residual.reshape(count, length, 2, length),
        preferred_element_type=jnp.float32,
    ).astype(jnp.bfloat16)
    near_field = jnp.einsum(
        "syab,ybd->sad", back_half, backward_right, preferred_element_type=jnp.float32
    )
    grad_real = near_field[:, :, :length]
    grad_imag = near_field[:, :, length:]
    object_real = wave_real * grad_real + wave_imag * grad_imag
    object_imag = wave_real * grad_imag - wave_imag * grad_real
    cells = jnp.stack([object_imag, -object_real], axis=1)
    probe_term = jnp.stack(
        [
            jnp.sum(trans_real * grad_real + trans_imag * grad_imag, axis=0),
            jnp.sum(trans_real * grad_imag - trans_imag * grad_real, axis=0),
        ]
    )

    def add_window(index, canvas_now):
        where = (zero_index, row_begin[index], col_begin[index])
        piece = lax.dynamic_slice(canvas_now, where, (2, length, length))
        return lax.dynamic_update_slice(canvas_now, piece + cells[index], where)

    canvas = jnp.zeros((2, rows_local + length, cols_local + length), jnp.float32)
    canvas = lax.fori_loop(0, count, add_window, canvas)
    summed, probe_part, misfit_part = lax.psum((canvas, probe_term, misfit), "beam")
    probe_total, misfit_total = lax.psum((probe_part, misfit_part), ("row", "col"))
    gradient = fold_rims(summed, half)
    square_sum = lax.psum(jnp.sum(gradient * gradient), ("row", "col"))
    plane_devices = lax.axis_size("row") * lax.axis_size("col")
    mean_square = square_sum / (2 * rows_local * cols_local * plane_devices)
    factor = jnp.minimum(1.0, 0.5 / jnp.sqrt(mean_square + 1e-06))
    total = plane_devices * lax.axis_size("beam") * count
    return (gradient * factor, probe_total / total, misfit_total / (total * length * length))


def solution(mesh):
    in_specs = (
        P("beam", "row", "col"),
        P("beam", "row", "col"),
        P(),
        P("row", "col", "beam", None, None),
        P("row", "col", "beam"),
        P("row", "col", "beam"),
    )
    out_specs = (P(None, "row", "col"), P(), P())
    return jax.shard_map(local, mesh=mesh, in_specs=in_specs, out_specs=out_specs, check_vma=False)
```

profile of v0, /device:TPU:0, one launch (start us, length us, event | category | flops | bytes accessed | tf_op | source)
XLA Modules:
  0.0 417.0 jit_solution(9984468014252012961)
XLA Ops:
  13.5 43.8 %all-reduce.13.cloned.1.call-done = (f32[1,256,128]{2,1,0:T(8,128)}, f32[1,256,128]{2,1,0:T(8,128)}) async-done(((f32[1,256,128]{2,1,0:T(8,128)}, f32[1,256,128]{2,1,0:T(8,128)}), (f32[1,256,128]{2,1,0:T(8,128)}, f32[1,256,128]{2,1,0:T(8,128)})) %all-reduce.13.cloned.1.call-update) | async-done | bytes 262160 | tf_op jit(solution)/shard_map/psum | solution.py:66
  59.2 3.4 collective-permute-start
  66.0 3.4 collective-permute-done.1
  75.9 22.0 %while.15 = (s32[]{:T(128)}, f32[2,512,384]{2,1,0:T(8,128)S(1)}, s32[8,3]{0,1:T(4,128)S(1)}, f32[8,2,256,256]{3,2,0,1:T(8,128)}, s32[]{:T(128)}) while((s32[]{:T(128)}, f32[2,512,384]{2,1,0:T(8,128)S(1)}, s32[8,3]{0,1:T(4,128)S(1)}, f32[8,2,256,256]{3,2,0,1:T(8,128)}, s32[]{:T(128)}) %tuple.69), condition=%wide.while_cond, body=%wide.while_body.sunk | while | flops 2 | bytes 1050217 | solution.py:72
  76.5 2.1 bitcast_dynamic-update-slice_fusion.2
  82.0 2.1 bitcast_dynamic-update-slice_fusion.2
  84.7 2.2 bitcast_dynamic-update-slice_fusion.2
  87.5 2.1 bitcast_dynamic-update-slice_fusion.2
  90.2 2.1 bitcast_dynamic-update-slice_fusion.2
  93.0 2.2 bitcast_dynamic-update-slice_fusion.2
  97.9 9.9 %subtract_convert_fusion = (bf16[8,1,256,256]{3,2,0,1:T(8,128)(2,1)}, f32[8,1,256,256]{3,2,0,1:T(8,128)S(1)}, f32[8,1,256,256]{3,2,0,1:T(8,128)S(1)}) fusion(f32[256,256]{1,0:T(8,128)S(1)} %get-tuple-element.153, f32[256,256]{1,0:T(8,128)S(1)} %get-tuple-element.152, f32[8,2,256,256]{3,2,0,1:T(8,128)} %get-tuple-element.105), kind=kLoop, calls=%fused_computation.40 | loop fusion | flops 3670016 | bytes 9961472 | tf_op jit(solution)/shard_map/convert.1
  109.5 6.0 %convolution_bitcast_fusion.1 = f32[8,256,512]{2,1,0:T(8,128)} fusion(bf16[1,2,256,256]{3,2,1,0:T(8,128)(2,1)} %get-tuple-element.159, bf16[1,2,256,256]{3,2,1,0:T(8,128)(2,1)} %get-tuple-element.166, bf16[1,256,512]{2,1,0:T(8,128)(2,1)S(1)} %copy-done.6, bf16[1,256,512]{2,1,0:T(8,128)(2,1)S(1)} %copy-done.7, bf16[8,1,256,256]{3,2,0,1:T(8,128)(2,1)} %add_convert_fusion, ...), kind=kOutput, calls=%fused_computation.11 | convolution fusion | flops 2150891520 | bytes 7340032 | tf_op jit(solution)/shard_map/sxab,xbd->sad/dot_general | solution.py:105
  115.5 4.5 %fusion.3 = (f32[]{:T(128)}, f32[8,256,256]{2,1,0:T(8,128)S(1)}) fusion(bf16[1,1,8,256,256]{4,3,2,1,0:T(8,128)(2,1)} %param.11, f32[8,256,512]{2,1,0:T(8,128)} %convolution_bitcast_fusion.1), kind=kLoop, calls=%fused_computation.14 | loop fusion | flops 5242879 | bytes 7340036 | tf_op jit(solution)/shard_map/reduce_sum | solution.py:112
  121.9 4.0 copy.18
  125.9 5.9 %convolution_bitcast_fusion = f32[8,256,512]{2,1,0:T(8,128)} fusion(bf16[8,256,2,256,1]{1,3,2,4,0:T(8,128)(2,1)} %bitcast.155, bf16[1,2,256,256]{3,2,1,0:T(8,128)(2,1)} %get-tuple-element.167, bf16[1,2,256,256]{3,2,1,0:T(8,128)(2,1)S(1)} %copy-done.5, bf16[1,256,512]{2,1,0:T(8,128)(2,1)S(1)} %copy-done.4, bf16[1,256,512]{2,1,0:T(8,128)(2,1)S(1)} %get-tuple-element.154), kind=kOutput, calls=%fused_computation.10 | convolution fusion | flops 2149842944 | bytes 7340032 | tf_op jit(solution)/shard_map/syab,ybd->sad/dot_general | solution.py:121
  131.8 4.4 %fusion.11 = (f32[256,256]{1,0:T(8,128)S(1)}, f32[256,256]{1,0:T(8,128)S(1)}, f32[8,1,256,256]{3,2,0,1:T(8,128)S(1)}, f32[8,1,256,256]{3,2,0,1:T(8,128)S(1)}) fusion(f32[8,1,256,256]{3,2,0,1:T(8,128)S(1)} %get-tuple-element.138, f32[8,1,256,256]{3,2,0,1:T(8,128)} %copy-done.1, f32[8,256,512]{2,1,0:T(8,128)} %convolution_bitcast_fusion, ...), kind=kLoop, calls=%fused_computation.29 | loop fusion | flops 10878976 | bytes 13631488 | tf_op jit(solution)/shard_map/reduce_sum | solution.py:131
  136.2 2.2 pad_maximum_fusion
  138.5 117.0 %while.14 = (s32[]{:T(128)}, f32[2,512,384]{2,1,0:T(8,128)S(1)}, s32[8]{0:T(128)S(1)}, s32[8]{0:T(128)S(1)}, f32[8,2,256,256]{3,2,0,1:T(8,128)}, /*index=5*/s32[]{:T(128)}, s32[]{:T(128)}, s32[]{:T(128)}, s32[]{:T(128)}) while((s32[]{:T(128)}, f32[2,512,384]{2,1,0:T(8,128)S(1)}, s32[8]{0:T(128)S(1)}, s32[8]{0:T(128)S(1)}, ...), condition=%wide.region_5.6_spmd, body=%wide.region_4.5_spmd.sunk | while | flops 131080 | bytes 2621641 | solution.py:142
  144.8 8.4 %dynamic_update_slice.8 = f32[2,512,384]{2,1,0:T(8,128)S(1)} dynamic-update-slice(f32[2,512,384]{2,1,0:T(8,128)S(1)} %get-tuple-element.259, f32[2,256,256]{2,1,0:T(8,128)S(1)} %bitcast_add_fusion.2, s32[]{:T(128)} %constant.69.clone.1..sunk, s32[]{:T(128)S(6)} %select_n.125, s32[]{:T(128)S(6)} %select_n.126) | dynamic-update-slice | bytes 1048580 | tf_op jit(solution)/shard_map/while/body/eval_jaxpr/dynamic_update_slice | solution.py:139
  159.6 9.1 %dynamic_update_slice.8 = f32[2,512,384]{2,1,0:T(8,128)S(1)} dynamic-update-slice(f32[2,512,384]{2,1,0:T(8,128)S(1)} %get-tuple-element.259, f32[2,256,256]{2,1,0:T(8,128)S(1)} %bitcast_add_fusion.2, s32[]{:T(128)} %constant.69.clone.1..sunk, s32[]{:T(128)S(6)} %select_n.125, s32[]{:T(128)S(6)} %select_n.126) | dynamic-update-slice | bytes 1048580 | tf_op jit(solution)/shard_map/while/body/eval_jaxpr/dynamic_update_slice | solution.py:139
  175.1 8.6 %dynamic_update_slice.8 = f32[2,512,384]{2,1,0:T(8,128)S(1)} dynamic-update-slice(f32[2,512,384]{2,1,0:T(8,128)S(1)} %get-tuple-element.259, f32[2,256,256]{2,1,0:T(8,128)S(1)} %bitcast_add_fusion.2, s32[]{:T(128)} %constant.69.clone.1..sunk, s32[]{:T(128)S(6)} %select_n.125, s32[]{:T(128)S(6)} %select_n.126) | dynamic-update-slice | bytes 1048580 | tf_op jit(solution)/shard_map/while/body/eval_jaxpr/dynamic_update_slice | solution.py:139
  190.0 7.9 %dynamic_update_slice.8 = f32[2,512,384]{2,1,0:T(8,128)S(1)} dynamic-update-slice(f32[2,512,384]{2,1,0:T(8,128)S(1)} %get-tuple-element.259, f32[2,256,256]{2,1,0:T(8,128)S(1)} %bitcast_add_fusion.2, s32[]{:T(128)} %constant.69.clone.1..sunk, s32[]{:T(128)S(6)} %select_n.125, s32[]{:T(128)S(6)} %select_n.126) | dynamic-update-slice | bytes 1048580 | tf_op jit(solution)/shard_map/while/body/eval_jaxpr/dynamic_update_slice | solution.py:139
  204.3 7.6 %dynamic_update_slice.8 = f32[2,512,384]{2,1,0:T(8,128)S(1)} dynamic-update-slice(f32[2,512,384]{2,1,0:T(8,128)S(1)} %get-tuple-element.259, f32[2,256,256]{2,1,0:T(8,128)S(1)} %bitcast_add_fusion.2, s32[]{:T(128)} %constant.69.clone.1..sunk, s32[]{:T(128)S(6)} %select_n.125, s32[]{:T(128)S(6)} %select_n.126) | dynamic-update-slice | bytes 1048580 | tf_op jit(solution)/shard_map/while/body/eval_jaxpr/dynamic_update_slice | solution.py:139
  218.2 8.4 %dynamic_update_slice.8 = f32[2,512,384]{2,1,0:T(8,128)S(1)} dynamic-update-slice(f32[2,512,384]{2,1,0:T(8,128)S(1)} %get-tuple-element.259, f32[2,256,256]{2,1,0:T(8,128)S(1)} %bitcast_add_fusion.2, s32[]{:T(128)} %constant.69.clone.1..sunk, s32[]{:T(128)S(6)} %select_n.125, s32[]{:T(128)S(6)} %select_n.126) | dynamic-update-slice | bytes 1048580 | tf_op jit(solution)/shard_map/while/body/eval_jaxpr/dynamic_update_slice | solution.py:139
  233.0 7.1 %dynamic_update_slice.8 = f32[2,512,384]{2,1,0:T(8,128)S(1)} dynamic-update-slice(f32[2,512,384]{2,1,0:T(8,128)S(1)} %get-tuple-element.259, f32[2,256,256]{2,1,0:T(8,128)S(1)} %bitcast_add_fusion.2, s32[]{:T(128)} %constant.69.clone.1..sunk, s32[]{:T(128)S(6)} %select_n.125, s32[]{:T(128)S(6)} %select_n.126) | dynamic-update-slice | bytes 1048580 | tf_op jit(solution)/shard_map/while/body/eval_jaxpr/dynamic_update_slice | solution.py:139
  246.4 9.0 %dynamic_update_slice.8 = f32[2,512,384]{2,1,0:T(8,128)S(1)} dynamic-update-slice(f32[2,512,384]{2,1,0:T(8,128)S(1)} %get-tuple-element.259, f32[2,256,256]{2,1,0:T(8,128)S(1)} %bitcast_add_fusion.2, s32[]{:T(128)} %constant.69.clone.1..sunk, s32[]{:T(128)S(6)} %select_n.125, s32[]{:T(128)S(6)} %select_n.126) | dynamic-update-slice | bytes 1048580 | tf_op jit(solution)/shard_map/while/body/eval_jaxpr/dynamic_update_slice | solution.py:139
  256.9 71.4 %all-reduce.11.cloned.1.call-done = (f32[2,512,384]{2,1,0:T(8,128)}, f32[2,256,256]{2,1,0:T(8,128)}) async-done(((f32[2,512,384]{2,1,0:T(8,128)}, f32[2,256,256]{2,1,0:T(8,128)}), (f32[2,512,384]{2,1,0:T(8,128)}, f32[2,256,256]{2,1,0:T(8,128)})) %all-reduce.11.cloned.1.call-update) | async-done | bytes 2097168 | tf_op jit(solution)/shard_map/psum | solution.py:143
  330.9 3.1 collective-permute-start.5
  337.9 4.6 %collective-permute-start.7 = (f32[2,128,128]{2,1,0:T(8,128)S(1)}, f32[2,128,128]{2,1,0:T(8,128)S(1)}, u32[]{:S(2)}, u32[]{:S(2)}) collective-permute-start(f32[2,128,128]{2,1,0:T(8,128)S(1)} %get-tuple-element.151), channel_id=1, source_target_pairs={{0,2},{2,4},{4,6},{1,3},{3,5},{5,7},{8,10},{10,12},{12,14},{9,11},... | collective-permute-start | bytes 393224 | tf_op jit(solution)/shard_map/ppermute | solution.py:12
  342.5 9.4 %psum.62 = f32[]{:T(128)} all-reduce(f32[]{:T(128)} %get-tuple-element.146), channel_id=1, replica_groups=mesh['beam'=4,'row'=4,'col'=2] {'beam'}, use_global_device_ids=true, to_apply=%region_14.15 | all-reduce | flops 1 | bytes 8 | tf_op jit(solution)/shard_map/psum | solution.py:143
  352.6 38.5 %all-reduce.9.cloned.1.call-done = f32[2,256,256]{2,1,0:T(8,128)} async-done(((f32[2,256,256]{2,1,0:T(8,128)}), f32[2,256,256]{2,1,0:T(8,128)}) %all-reduce.9.cloned.1.call-update) | async-done | bytes 524304 | tf_op jit(solution)/shard_map/psum | solution.py:144
  392.9 14.3 %all-reduce.2 = (f32[]{:T(128)}, f32[]{:T(128)}) all-reduce(f32[]{:T(128)} %multiply_reduce_fusion, f32[]{:T(128)} %psum.62), channel_id=1, replica_groups=mesh['beam'=4,'row'=4,'col'=2] {'row','col'}, use_global_device_ids=true, to_apply=%region_8.9 | all-reduce | flops 2 | bytes 16 | tf_op jit(solution)/shard_map/psum | solution.py:146
  (108 shorter events, 61.3 us)
Async XLA Ops:
  7.2 6.3 %copy-start.8 = (s32[1,1,8]{2,1,0:T(1,128)S(1)}, s32[1,1,8]{2,1,0:T(1,128)}, u32[]{:S(2)}) copy-start(s32[1,1,8]{2,1,0:T(1,128)} %param.12) | copy-start | bytes 100
  7.2 6.3 %copy-start.9 = (s32[1,1,8]{2,1,0:T(1,128)S(1)}, s32[1,1,8]{2,1,0:T(1,128)}, u32[]{:S(2)}) copy-start(s32[1,1,8]{2,1,0:T(1,128)} %param.13) | copy-start | bytes 100
  7.2 50.1 %all-reduce.13.cloned.1.call-start = ((), (), s32[]{:S(2)}) async-start(), calls=%async_computation.2 | async-start | bytes 524288 | tf_op jit(solution)/shard_map/psum | solution.py:66
  11.3 317.0 %all-reduce.11.cloned.1.call-start = ((), (), s32[]{:S(2)}) async-start(), calls=%async_computation.1 | async-start | bytes 4194304 | tf_op jit(solution)/shard_map/psum | solution.py:143
  59.2 6.8 %collective-permute-start = (f32[2,128,128]{2,1,0:T(8,128)S(1)}, f32[2,128,128]{2,1,0:T(8,128)S(1)}, u32[]{:S(2)}, u32[]{:S(2)}) collective-permute-start(f32[2,128,128]{2,1,0:T(8,128)S(1)} %get-tuple-element.162), channel_id=1, source_target_pairs={{0,2},{2,4},{4,6},{1,3},{3,5},{5,7},{8,10},{10,12},{12,14},{9,11},... | collective-permute-start | bytes 393224 | tf_op jit(solution)/shard_map/ppermute | solution.py:23
  62.6 6.9 %collective-permute-start.1 = (f32[2,128,128]{2,1,0:T(8,128)S(1)}, f32[2,128,128]{2,1,0:T(8,128)S(1)}, u32[]{:S(2)}, u32[]{:S(2)}) collective-permute-start(f32[2,128,128]{2,1,0:T(8,128)S(1)} %get-tuple-element.163), channel_id=1, source_target_pairs={{2,0},{4,2},{6,4},{3,1},{5,3},{7,5},{10,8},{12,10},{14,12},{11,9},... | collective-permute-start | bytes 393224 | tf_op jit(solution)/shard_map/ppermute | solution.py:25
  64.9 9.4 %copy-start.3 = (f32[2,256,256]{2,1,0:T(8,128)S(1)}, f32[2,256,256]{2,1,0:T(8,128)}, u32[]{:S(2)}) copy-start(f32[2,256,256]{2,1,0:T(8,128)} %param.10) | copy-start | bytes 1572868
  69.5 4.9 %collective-permute-start.2 = (f32[2,512,128]{2,1,0:T(8,128)S(1)}, f32[2,512,128]{2,1,0:T(8,128)S(1)}, u32[]{:S(2)}, u32[]{:S(2)}) collective-permute-start(f32[2,512,128]{2,1,0:T(8,128)S(1)} %pad_maximum_fusion.2), channel_id=1, source_target_pairs={{0,1},{2,3},{4,5},{6,7},{8,9},{10,11},{12,13},{14,15},{16,17},{18,... | collective-permute-start | bytes 1572872 | tf_op jit(solution)/shard_map/ppermute | solution.py:23
  70.8 3.9 collective-permute-start.3
  107.8 1.7 copy-start.1
  107.8 1.7 copy-start.6
  107.8 1.7 copy-start.7
  115.5 4.5 %copy-start.2 = (f32[8,256,512]{2,1,0:T(8,128)S(1)}, f32[8,256,512]{2,1,0:T(8,128)}, u32[]{:S(2)}) copy-start(f32[8,256,512]{2,1,0:T(8,128)} %convolution_bitcast_fusion.1) | copy-start | bytes 12582916
  121.9 4.0 copy-start.4
  121.9 4.0 copy-start.5
  255.4 1.4 copy-start
  256.8 134.2 %all-reduce.9.cloned.1.call-start = ((), (), s32[]{:S(2)}) async-start(), calls=%async_computation | async-start | bytes 1048576 | tf_op jit(solution)/shard_map/psum | solution.py:144
  329.6 4.4 %collective-permute-start.4 = (f32[2,512,128]{2,1,0:T(8,128)S(1)}, f32[2,512,128]{2,1,0:T(8,128)S(1)}, u32[]{:S(2)}, u32[]{:S(2)}) collective-permute-start(f32[2,512,128]{2,1,0:T(8,128)S(1)} %get-tuple-element.148), channel_id=1, source_target_pairs={{1,0},{3,2},{5,4},{7,6},{9,8},{11,10},{13,12},{15,14},{17,16},{19,... | collective-permute-start | bytes 1572872 | tf_op jit(solution)/shard_map/ppermute | solution.py:12
  330.9 4.6 %collective-permute-start.5 = (f32[2,512,128]{2,1,0:T(8,128)S(1)}, f32[2,512,128]{2,1,0:T(8,128)S(1)}, u32[]{:S(2)}, u32[]{:S(2)}) collective-permute-start(f32[2,512,128]{2,1,0:T(8,128)S(1)} %get-tuple-element.149), channel_id=1, source_target_pairs={{0,1},{2,3},{4,5},{6,7},{8,9},{10,11},{12,13},{14,15},{16,17},{18,... | collective-permute-start | bytes 1572872 | tf_op jit(solution)/shard_map/ppermute | solution.py:12
  336.6 15.3 %collective-permute-start.6 = (f32[2,128,128]{2,1,0:T(8,128)S(1)}, f32[2,128,128]{2,1,0:T(8,128)S(1)}, u32[]{:S(2)}, u32[]{:S(2)}) collective-permute-start(f32[2,128,128]{2,1,0:T(8,128)S(1)} %get-tuple-element.150), channel_id=1, source_target_pairs={{2,0},{4,2},{6,4},{3,1},{5,3},{7,5},{10,8},{12,10},{14,12},{11,9},... | collective-permute-start | bytes 393224 | tf_op jit(solution)/shard_map/ppermute | solution.py:12
  337.9 14.0 %collective-permute-start.7 = (f32[2,128,128]{2,1,0:T(8,128)S(1)}, f32[2,128,128]{2,1,0:T(8,128)S(1)}, u32[]{:S(2)}, u32[]{:S(2)}) collective-permute-start(f32[2,128,128]{2,1,0:T(8,128)S(1)} %get-tuple-element.151), channel_id=1, source_target_pairs={{0,2},{2,4},{4,6},{1,3},{3,5},{5,7},{8,10},{10,12},{12,14},{9,11},... | collective-permute-start | bytes 393224 | tf_op jit(solution)/shard_map/ppermute | solution.py:12
Sparse Core Ops, SparseCore 0:
  11.5 45.8 all-reduce.12
  257.0 71.3 all-reduce.10
  334.1 56.8 all-reduce.8
where the time goes:
time: 419 us; the launch traced here: 417 us
  waiting for transfers between devices  159 us (38%)
  local copies, waits for them, and re-layouts  105 us (25%)
  other arithmetic  51.2 us (12%)
  loops' own time  31.3 us (7%)
  blocking collectives  23.7 us (6%)
  starting transfers between devices  17.8 us (4%)
  between operations  16.5 us (4%)
  matrix products  11.9 us (3%)
    psum x1, waiting for transfers between devices, local(): lax.psum((canvas, probe_term, misfit), 'beam')  71.4 us
    dynamic_update_slice x8, local copies, waits for them, and re-layouts, add_window(): return lax.dynamic_update_slice(canvas_now, piece + cells[index], where)  66.1 us
    psum x1, waiting for transfers between devices, local(): phase_sum, absorb_sum = lax.psum((phase_part, absorb_part), 'beam')  43.8 us
    psum x1, waiting for transfers between devices, local(): lax.psum((probe_part, misfit_part), ('row', 'col'))  38.5 us
    another operation x1, loops' own time, local(): canvas = lax.fori_loop(0, count, add_window, canvas)  31.3 us
    gather x24, local copies, waits for them, and re-layouts  21.9 us
    psum x1, blocking collectives, local(): square_sum = lax.psum(jnp.sum(gradient * gradient), ('row', 'col'))  14.3 us
    another operation x2, other arithmetic  11.4 us
  transfers between devices with their start and end apart: 11, of which 6 were waited for; matrix products, arithmetic and copies ran while one was open for 2% of the time, Pallas kernels for 0%

commit v1 on v0

v1 whole, which is shorter than its diff:
```python
import functools
import math

import jax
import jax.numpy as jnp
import numpy as np
from jax import lax
from jax.experimental import pallas as pl
from jax.experimental.pallas import tpu as pltpu
from jax.sharding import PartitionSpec as P

LANES = 128
SUBS = 8
CHUNK = 32
VMEM = pl.BlockSpec(memory_space=pltpu.VMEM)
SMEM = pl.BlockSpec(memory_space=pltpu.SMEM)
F32 = jnp.float32
BF16 = jnp.bfloat16


def dft_blocks(length):
    indices = np.arange(length, dtype=np.int64)
    product = (indices[:, None] * indices[None, :] % length).astype(np.float32)
    angles = (product * np.float32(2.0 * math.pi / length)).astype(np.float64)
    factor = np.float32(1.0 / math.sqrt(length))
    real = (np.cos(angles).astype(np.float32) * factor).astype(jnp.bfloat16)
    imag = (-np.sin(angles).astype(np.float32) * factor).astype(jnp.bfloat16)
    forward = np.block([[real, -imag], [imag, real]])
    backward = np.block([[real, imag], [-imag, real]])
    return forward.astype(jnp.bfloat16), backward.astype(jnp.bfloat16)


def exchange(value, axis, mask):
    count = lax.axis_size(axis)
    return lax.ppermute(value, axis, [(i, i ^ mask) for i in range(count)])


def rows_of(index, size):
    return pl.ds(pl.multiple_of(index * size, size), size)


def sum_kernel(beams, spot_ref, phase_ref, absorb_ref, *out_refs):
    part = phase_ref.shape[1] // beams
    for k in range(beams):
        where = rows_of(jnp.bitwise_xor(spot_ref[0], k), part)
        for comp, ref in enumerate((phase_ref, absorb_ref)):
            total = ref[0, where, :].astype(F32)
            for d in range(1, ref.shape[0]):
                total = total + ref[d, where, :].astype(F32)
            out_refs[k][comp] = total


def wave_kernel(beams, cols, count, length, *refs):
    spot_ref, row_ref, col_ref = refs[:3]
    mid_refs = refs[3 : 3 + beams]
    left_refs = refs[3 + beams : 3 + 2 * beams]
    right_refs = refs[3 + 2 * beams : 3 + 3 * beams]
    probe_ref, amp_ref, forward_ref, backward_ref = refs[3 + 3 * beams : 7 + 3 * beams]
    sends = 1 if cols == 2 else 2
    outs = refs[7 + 3 * beams : 8 + 3 * beams + sends]
    cells, canvas, probe_sum, miss, trans, psi, half_wave, far, chi, back, near = refs[
        8 + 3 * beams + sends :
    ]
    part = mid_refs[0].shape[1]
    tall = cells.shape[2]
    beam, col = spot_ref[0], spot_ref[2]
    has_left, has_right = col > 0, col < cols - 1
    for k in range(beams):
        quarter = jnp.bitwise_xor(beam, k)
        spots = (quarter + beams // 2, lax.rem(quarter + 3 * beams // 2, 2 * beams))
        for which, at in enumerate(spots):
            where = rows_of(at, part)
            for comp in range(2):
                outside = 1.0 - comp
                source = 2 * which + comp
                cells[comp, 0, where, :] = jnp.where(has_left, left_refs[k][source], outside)
                cells[comp, 1, where, :] = mid_refs[k][source]
                cells[comp, 2, where, :] = jnp.where(has_right, right_refs[k][source], outside)
    canvas[...] = jnp.zeros_like(canvas)
    probe_sum[...] = jnp.zeros_like(probe_sum)
    miss[...] = jnp.zeros_like(miss)
    lane = lax.broadcasted_iota(jnp.int32, (CHUNK, LANES), 1)
    chunks = length // CHUNK

    def window(s, carry):
        row_at, col_at = row_ref[s], col_ref[s]
        back_shift = lax.rem(LANES - col_at, LANES)
        low = lane < LANES - col_at
        for i in range(chunks):
            here = pl.ds(i * CHUNK, CHUNK)
            there = pl.ds(row_at + i * CHUNK, CHUNK)
            pieces = []
            for comp in range(2):
                turned = [
                    pltpu.roll(cells[comp, j, there, :], back_shift, 1) for j in range(3)
                ]
                pieces.append([jnp.where(low, turned[j], turned[j + 1]) for j in range(2)])
            for j in range(2):
                lanes = pl.ds(j * LANES, LANES)
                real, imag = pieces[0][j], pieces[1][j]
                trans[0, j, here, :] = real
                trans[1, j, here, :] = imag
                probe_real = probe_ref[0, here, lanes]
                probe_imag = probe_ref[1, here, lanes]
                psi[here, lanes] = (probe_real * real - probe_imag * imag).astype(BF16)
                psi[pl.ds(length + i * CHUNK, CHUNK), lanes] = (
                    probe_real * imag + probe_imag * real
                ).astype(BF16)
        result = jnp.dot(forward_ref[...], psi[...], preferred_element_type=F32).astype(BF16)
        half_wave[:, :length] = result[:length]
        half_wave[:, length:] = result[length:]
        far[...] = jnp.dot(half_wave[...], backward_ref[...], preferred_element_type=F32)
        for i in range(chunks):
            here = pl.ds(i * CHUNK, CHUNK)
            real, imag = far[here, :length], far[here, length:]
            amplitude = amp_ref[s, here, :].astype(F32)
            power = real * real + imag * imag
            off = jnp.sqrt(power) - amplitude
            wide = off * off
            wide = wide[:, :LANES] + wide[:, LANES:]
            miss[...] += wide.reshape(CHUNK // SUBS, SUBS, LANES).sum(0)
            ratio = 1.0 - amplitude * lax.rsqrt(jnp.maximum(power, 0.25))
            chi[here, :] = (real * ratio).astype(BF16)
            chi[pl.ds(length + i * CHUNK, CHUNK), :] = (imag * ratio).astype(BF16)
        result = jnp.dot(backward_ref[...], chi[...], preferred_element_type=F32).astype(BF16)
        back[:, :length] = result[:length]
        back[:, length:] = result[length:]
        near[...] = jnp.dot(back[...], forward_ref[...], preferred_element_type=F32)
        high = lane >= col_at
        for i in range(chunks):
            here = pl.ds(i * CHUNK, CHUNK)
            there = pl.ds(row_at + i * CHUNK, CHUNK)
            turned = [[], []]
            for j in range(2):
                lanes = pl.ds(j * LANES, LANES)
                grad_real = near[here, lanes]
                grad_imag = near[here, pl.ds(length + j * LANES, LANES)]
                real, imag = trans[0, j, here, :], trans[1, j, here, :]
                probe_sum[0, j, here, :] += real * grad_real + imag * grad_imag
                probe_sum[1, j, here, :] += real * grad_imag - imag * grad_real
                probe_real = probe_ref[0, here, lanes]
                probe_imag = probe_ref[1, here, lanes]
                turned[0].append(
                    pltpu.roll(probe_real * grad_real + probe_imag * grad_imag, col_at, 1)
                )
                turned[1].append(
                    pltpu.roll(probe_real * grad_imag - probe_imag * grad_real, col_at, 1)
                )
            for comp in range(2):
                first, second = turned[comp]
                canvas[comp, 0, there, :] += jnp.where(high, first, 0.0)
                canvas[comp, 1, there, :] += jnp.where(high, second, first)
                canvas[comp, 2, there, :] += jnp.where(high, 0.0, second)
        return carry

    lax.fori_loop(0, count, window, 0)
    base = 2 * tall
    if cols == 2:
        tiles = (1, 2 * has_right.astype(jnp.int32))
        comps = ((col,), (1 - col,))
    else:
        tiles = (1, 0, 2)
        comps = ((0, 1), (), ())
    for out, tile, held in zip(outs, tiles, comps):
        for comp in range(2):
            out[pl.ds(comp * tall, tall), :] = canvas[comp, tile]
        for n, comp in enumerate(held):
            for j in range(2):
                out[pl.ds(base + (2 * n + j) * length, length), :] = probe_sum[comp, j]
        if held:
            out[pl.ds(base + 2 * len(held) * length, SUBS), :] = miss[...]


def split_kernel(beams, tall, length, *refs):
    spot_ref = refs[0]
    ins, outs = refs[1:-beams], refs[-beams:]
    part = tall // (2 * beams)
    strip = length // beams
    planes = (ins[0].shape[0] - 2 * tall - SUBS) // length

    def fetch(where):
        total = ins[0][where, :]
        for ref in ins[1:]:
            total = total + ref[where, :]
        return total

    for k in range(beams):
        quarter = jnp.bitwise_xor(spot_ref[0], k)
        spots = (quarter + beams // 2, lax.rem(quarter + 3 * beams // 2, 2 * beams))
        for which, at in enumerate(spots):
            for comp in range(2):
                where = pl.ds(pl.multiple_of(comp * tall + at * part, SUBS), part)
                outs[k][pl.ds((2 * which + comp) * part, part), :] = fetch(where)
        for n in range(planes):
            start = 2 * tall + n * length + quarter * strip
            where = pl.ds(pl.multiple_of(start, SUBS), strip)
            outs[k][pl.ds(4 * part + n * strip, strip), :] = fetch(where)
        where = pl.ds(2 * tall + planes * length, SUBS)
        outs[k][pl.ds(4 * part + planes * strip, SUBS), :] = fetch(where)


def final_kernel(beams, halves, planes, scale, total, *refs):
    spot_ref = refs[0]
    objects = refs[1 : 1 + beams]
    probes = [refs[1 + (1 + h) * beams : 1 + (2 + h) * beams] for h in range(halves)]
    squares_in = refs[1 + (1 + halves) * beams :][:-3]
    object_ref, probe_ref, loss_ref = refs[-3:]
    part = objects[0].shape[0] // 2
    strip = (probes[0][0].shape[0] - 2 * SUBS) // planes
    length = strip * beams
    miss_at = pl.ds(planes * strip, SUBS)
    square_at = pl.ds(planes * strip + SUBS, SUBS)

    def paired(refs_now, where):
        values = [ref[where, :] for ref in refs_now]
        while len(values) > 1:
            values = [values[i] + values[i + 1] for i in range(0, len(values), 2)]
        return values[0]

    if squares_in:
        squares = squares_in[0][...]
    else:
        squares = paired(probes[0], square_at)
        for more in probes[1:]:
            squares = squares + paired(more, square_at)
    mean_square = jnp.sum(squares, keepdims=True) * scale
    factor = jnp.minimum(1.0, 0.5 / jnp.sqrt(mean_square + 1e-06))
    loss = jnp.sum(probes[0][0][miss_at, :], keepdims=True) / (total * length * length)
    loss_ref[...] = jnp.broadcast_to(loss, loss_ref.shape)
    for k in range(beams):
        quarter = jnp.bitwise_xor(spot_ref[0], k)
        where = rows_of(quarter, part)
        for comp in range(2):
            object_ref[comp, where, :] = objects[k][pl.ds(comp * part, part), :] * factor
        where = rows_of(quarter, strip)
        for h in range(halves):
            for n in range(planes):
                comp = (jnp.bitwise_xor(spot_ref[2], h)) if halves == 2 else n // 2
                lanes = pl.ds((n % 2) * LANES, LANES)
                probe_ref[comp, where, lanes] = (
                    probes[h][k][pl.ds(n * strip, strip), :] * (1.0 / total)
                )


def call(kernel, shapes, scalars, arrays, scratch=(), flops=0):
    size = sum(a.size * a.dtype.itemsize for a in arrays)
    return pl.pallas_call(
        kernel,
        out_shape=[jax.ShapeDtypeStruct(s, F32) for s in shapes],
        in_specs=[SMEM] * len(scalars) + [VMEM] * len(arrays),
        out_specs=[VMEM] * len(shapes),
        scratch_shapes=list(scratch),
        compiler_params=pltpu.CompilerParams(vmem_limit_bytes=40 * 2**20),
        cost_estimate=pl.CostEstimate(flops=flops, bytes_accessed=size, transcendentals=0),
    )(*scalars, *arrays)


def local(phase_volume, absorb_volume, probe, amplitudes, scan_rows, scan_cols):
    length = probe.shape[1]
    count = scan_rows.shape[2]
    rows_local = phase_volume.shape[1]
    cols_local = phase_volume.shape[2]
    beams, rows, cols = (lax.axis_size(a) for a in ("beam", "row", "col"))
    assert cols_local == LANES and length == 2 * LANES and rows_local == length
    beam, row, col = (lax.axis_index(a) for a in ("beam", "row", "col"))
    spot = jnp.stack([beam, row, col]).astype(jnp.int32)
    part = rows_local // beams
    tall = rows_local + length
    others = range(1, beams)
    near_half = beams // 2

    def toward(step):
        pairs = []
        for b in range(beams):
            way = step if b >= near_half else -step
            for r in range(rows):
                if 0 <= r + way < rows:
                    pairs.append((b * rows + r, b * rows + r + way))
        return pairs

    sums = call(
        functools.partial(sum_kernel, beams),
        [(2, part, LANES)] * beams,
        [spot],
        [phase_volume, absorb_volume],
    )
    got = [sums[0]] + [exchange(sums[k], "beam", k) for k in others]
    total = functools.reduce(jnp.add, got)
    damping = jnp.exp(-total[1])
    trans = jnp.stack([damping * jnp.cos(total[0]), damping * jnp.sin(total[0])])
    halo = lax.ppermute(trans, ("beam", "row"), toward(1))
    inside = jnp.where(beam >= near_half, row > 0, row < rows - 1)
    outside = jnp.arange(2, dtype=jnp.int32).reshape(2, 1, 1) == 0
    halo = jnp.where(inside, halo, jnp.where(outside, 1.0, 0.0))
    own = jnp.concatenate([trans, halo])
    mids = [own] + [exchange(own, "beam", k) for k in others]
    if cols == 2:
        lefts = [exchange(x, "col", 1) for x in mids]
        rights = lefts
    else:
        lefts = [lax.ppermute(x, "col", [(i, i + 1) for i in range(cols - 1)]) for x in mids]
        rights = [lax.ppermute(x, "col", [(i + 1, i) for i in range(cols - 1)]) for x in mids]
    forward, backward = dft_blocks(length)
    paired = cols == 2
    planes = 2 if paired else 4
    deep = 2 * tall + planes * length + SUBS
    shapes = [(deep, LANES)] * 2 if paired else [(deep, LANES)] + [(2 * tall, LANES)] * 2
    outs = call(
        functools.partial(wave_kernel, beams, cols, count, length),
        shapes,
        [spot, scan_rows.reshape(count), scan_cols.reshape(count)],
        [*mids, *lefts, *rights, probe, amplitudes.reshape(count, length, length)]
        + [jnp.asarray(forward), jnp.asarray(backward)],
        [
            pltpu.VMEM((2, 3, tall, LANES), F32),
            pltpu.VMEM((2, 3, tall, LANES), F32),
            pltpu.VMEM((2, 2, length, LANES), F32),
            pltpu.VMEM((SUBS, LANES), F32),
            pltpu.VMEM((2, 2, length, LANES), F32),
            pltpu.VMEM((2 * length, length), BF16),
            pltpu.VMEM((length, 2 * length), BF16),
            pltpu.VMEM((length, 2 * length), F32),
            pltpu.VMEM((2 * length, length), BF16),
            pltpu.VMEM((length, 2 * length), BF16),
            pltpu.VMEM((length, 2 * length), F32),
        ],
        flops=count * 32 * length**3,
    )
    if paired:
        pieces = [outs[0], exchange(outs[1], "col", 1)]
    else:
        keep, to_left, to_right = outs
        edge = lax.ppermute(to_left, "col", [(i + 1, i) for i in range(cols - 1)])
        edge = edge + lax.ppermute(to_right, "col", [(i, i + 1) for i in range(cols - 1)])
        rest = lax.psum(keep[2 * tall :], "col")
        pieces = [jnp.concatenate([keep[: 2 * tall] + edge, rest])]
    strip = length // beams
    flat = 4 * part + planes * strip + SUBS
    split = call(
        functools.partial(split_kernel, beams, tall, length),
        [(flat, LANES)] * beams,
        [spot],
        pieces,
    )

    def butterfly(values):
        while len(values) > 1:
            values = [values[i] + values[i + 1] for i in range(0, len(values), 2)]
        return values[0]

    got = [split[0]] + [exchange(split[k], "beam", k) for k in others]
    summed = butterfly(got)
    halo = lax.ppermute(summed[2 * part : 4 * part], ("beam", "row"), toward(-1))
    whole = summed[: 2 * part] + halo
    real, imag = whole[:part], whole[part:]
    grad_phase = trans[0] * imag - trans[1] * real
    grad_absorb = -(trans[0] * real + trans[1] * imag)
    squares = grad_phase * grad_phase + grad_absorb * grad_absorb
    squares = squares.reshape(part // SUBS, SUBS, LANES).sum(0)
    gradient = jnp.concatenate([grad_phase, grad_absorb])
    objects = [gradient] + [exchange(gradient, "beam", k) for k in others]
    carried = jnp.concatenate([summed[4 * part :], squares])
    carried = butterfly([carried] + [exchange(carried, "row", k) for k in range(1, rows)])
    probes = [carried] + [exchange(carried, "beam", k) for k in others]
    operands = objects + probes
    if paired:
        operands = operands + [exchange(x, "col", 1) for x in probes]
    else:
        at = planes * strip + SUBS
        operands = operands + [lax.psum(butterfly([x[at:] for x in probes]), "col")]
    plane_devices = rows * cols
    objects_step, probe_gradient, loss = call(
        functools.partial(
            final_kernel,
            beams,
            2 if paired else 1,
            planes,
            1.0 / (2 * rows_local * cols_local * plane_devices),
            float(plane_devices * beams * count),
        ),
        [(2, rows_local, cols_local), (2, length, length), (1, 1)],
        [spot],
        operands,
    )
    return objects_step, probe_gradient, loss[0, 0]


def solution(mesh):
    in_specs = (
        P("beam", "row", "col"),
        P("beam", "row", "col"),
        P(),
        P("row", "col", "beam", None, None),
        P("row", "col", "beam"),
        P("row", "col", "beam"),
    )
    out_specs = (P(None, "row", "col"), P(), P())
    return jax.shard_map(local, mesh=mesh, in_specs=in_specs, out_specs=out_specs, check_vma=False)
```

time: 419 us -> 92.9 us (0.22)
  waiting for transfers between devices: 159 us -> 39.5 us
  local copies, waits for them, and re-layouts: 105 us -> 3.12 us
  other arithmetic: 51.2 us -> 0.44 us
  loops' own time: 31.3 us -> 0 us
  blocking collectives: 23.7 us -> 0 us
  Pallas kernels: 0 us -> 19.7 us
  between operations: 16.5 us -> 0.81 us
  matrix products: 11.9 us -> 0 us
  starting transfers between devices: 17.8 us -> 29.1 us
    psum x3 -> x0, waiting for transfers between devices: 154 us -> none  [the longest x1 71.4 us: local(): lax.psum((canvas, probe_term, misfit), 'beam')]
    dynamic_update_slice x8 -> x0, local copies, waits for them, and re-layouts: 66.1 us -> none  [add_window(): return lax.dynamic_update_slice(canvas_now, piece + cells[index], where)]
    ppermute x8 -> x29, waiting for transfers between devices: 5.29 us -> 39.5 us  [the longest x27 32.8 us: exchange(): return lax.ppermute(value, axis, [(i, i ^ mask) for i in range(count)])]
    another operation x2 -> x0, loops' own time: 31.3 us -> none  [the longest x1 31.3 us: local(): canvas = lax.fori_loop(0, count, add_window, canvas)]
    psum x2 -> x0, blocking collectives: 23.7 us -> none  [the longest x1 14.3 us: local(): square_sum = lax.psum(jnp.sum(gradient * gradient), ('row', 'col'))]
    gather x24 -> x0, local copies, waits for them, and re-layouts: 21.9 us -> none
    pallas_call x0 -> x4, Pallas kernels: none -> 19.7 us  [call(): pl.pallas_call(kernel, out_shape=[jax.ShapeDtypeStruct(s, F32) for s in s...]
    another operation x6 -> x2, other arithmetic: 16.4 us -> 0.08 us  [the longest x1 0.08 us: local(): spot = jnp.stack([beam, row, col]).astype(jnp.int32)]
  transfers between devices with their start and end apart: 11 -> 29, of which waited for: 6 -> 19; matrix products, arithmetic and copies ran while one was open for 2% -> 0% of each run, Pallas kernels for 0% -> 0%
where the time goes in v1:
time: 92.9 us; the launch traced here: 92.6 us
  waiting for transfers between devices  39.5 us (43%)
  starting transfers between devices  29.1 us (31%)
  Pallas kernels  19.7 us (21%)
  local copies, waits for them, and re-layouts  3.12 us (3%)
    ppermute x27, waiting for transfers between devices, exchange(): return lax.ppermute(value, axis, [(i, i ^ mask) for i in range(count)])  32.8 us
    ppermute x27, starting transfers between devices, exchange(): return lax.ppermute(value, axis, [(i, i ^ mask) for i in range(count)])  24.3 us
    pallas_call x4, Pallas kernels, call(): pl.pallas_call(kernel, out_shape=[jax.ShapeDtypeStruct(s, F32) for s in s...  19.7 us
    ppermute x1, waiting for transfers between devices, local(): halo = lax.ppermute(trans, ('beam', 'row'), toward(1))  4.85 us
    ppermute x1, starting transfers between devices, local(): halo = lax.ppermute(summed[2 * part:4 * part], ('beam', 'row'), toward(-1))  3.49 us
    unnamed x16, local copies, waits for them, and re-layouts  3.11 us
    ppermute x1, waiting for transfers between devices, local(): halo = lax.ppermute(summed[2 * part:4 * part], ('beam', 'row'), toward(-1))  1.87 us
  transfers between devices with their start and end apart: 29, of which 19 were waited for; matrix products, arithmetic and copies ran while one was open for 0% of the time, Pallas kernels for 0%

profile of v1, /device:TPU:0, one launch (start us, length us, event | category | flops | bytes accessed | tf_op | source)
XLA Modules:
  0.0 92.6 jit_solution(7675887426603860999)
XLA Ops:
  0.7 1.2 %copy-done = bf16[16,256,128]{2,1,0:T(8,128)(2,1)S(1)} copy-done((bf16[16,256,128]{2,1,0:T(8,128)(2,1)S(1)}, bf16[16,256,128]{2,1,0:T(8,128)(2,1)}, u32[]{:S(2)}) %copy-start) | copy-done | bytes 1048600
  1.9 1.2 %copy-done.1 = bf16[16,256,128]{2,1,0:T(8,128)(2,1)S(1)} copy-done((bf16[16,256,128]{2,1,0:T(8,128)(2,1)S(1)}, bf16[16,256,128]{2,1,0:T(8,128)(2,1)}, u32[]{:S(2)}) %copy-start.1) | copy-done | bytes 1048600
  3.2 0.8 shard_map.103
  4.0 3.0 %collective-permute-start = (f32[2,64,128]{2,1,0:T(8,128)S(1)}, f32[2,64,128]{2,1,0:T(8,128)S(1)}, u32[]{:S(2)}, u32[]{:S(2)}) collective-permute-start(f32[2,64,128]{2,1,0:T(8,128)S(1)} %get-tuple-element.17), channel_id=1, source_target_pairs={{0,8},{8,0},{16,24},{24,16},{1,9},{9,1},{17,25},{25,17},{2,10},{10... | collective-permute-start | bytes 196616 | tf_op jit(solution)/shard_map/ppermute | solution.py:35
  7.0 1.5 %collective-permute-start.1 = (f32[2,64,128]{2,1,0:T(8,128)S(1)}, f32[2,64,128]{2,1,0:T(8,128)S(1)}, u32[]{:S(2)}, u32[]{:S(2)}) collective-permute-start(f32[2,64,128]{2,1,0:T(8,128)S(1)} %get-tuple-element.18), channel_id=1, source_target_pairs={{0,16},{8,24},{16,0},{24,8},{1,17},{9,25},{17,1},{25,9},{2,18},{10... | collective-permute-start | bytes 196616 | tf_op jit(solution)/shard_map/ppermute | solution.py:35
  9.4 1.9 %collective-permute-done.1 = f32[2,64,128]{2,1,0:T(8,128)S(1)} collective-permute-done((f32[2,64,128]{2,1,0:T(8,128)S(1)}, f32[2,64,128]{2,1,0:T(8,128)S(1)}, u32[]{:S(2)}, u32[]{:S(2)}) %collective-permute-start.1) | collective-permute-done | bytes 65568 | tf_op jit(solution)/shard_map/ppermute | solution.py:35
  11.3 2.4 %collective-permute-done.2 = f32[2,64,128]{2,1,0:T(8,128)S(1)} collective-permute-done((f32[2,64,128]{2,1,0:T(8,128)S(1)}, f32[2,64,128]{2,1,0:T(8,128)S(1)}, u32[]{:S(2)}, u32[]{:S(2)}) %collective-permute-start.2) | collective-permute-done | bytes 65568 | tf_op jit(solution)/shard_map/ppermute | solution.py:35
  13.9 1.3 %collective-permute-start.3 = (f32[2,64,128]{2,1,0:T(8,128)S(1)}, f32[2,64,128]{2,1,0:T(8,128)S(1)}, u32[]{:S(2)}, u32[]{:S(2)}) collective-permute-start(f32[2,64,128]{2,1,0:T(8,128)S(1)} %pad_maximum_fusion.2), channel_id=1, source_target_pairs={{2,0},{4,2},{6,4},{10,8},{12,10},{14,12},{16,18},{18,20},{20,22},{... | collective-permute-start | bytes 196616 | tf_op jit(solution)/shard_map/ppermute | solution.py:291
  15.2 4.8 %collective-permute-done.3 = f32[2,64,128]{2,1,0:T(8,128)S(1)} collective-permute-done((f32[2,64,128]{2,1,0:T(8,128)S(1)}, f32[2,64,128]{2,1,0:T(8,128)S(1)}, u32[]{:S(2)}, u32[]{:S(2)}) %collective-permute-start.3) | collective-permute-done | bytes 65568 | tf_op jit(solution)/shard_map/ppermute | solution.py:291
  20.2 2.0 %collective-permute-start.5 = (f32[4,64,128]{2,1,0:T(8,128)S(1)}, f32[4,64,128]{2,1,0:T(8,128)S(1)}, u32[]{:S(2)}, u32[]{:S(2)}) collective-permute-start(f32[4,64,128]{2,1,0:T(8,128)S(1)} %pad_maximum_fusion.refs_3_), channel_id=1, source_target_pairs={{0,16},{8,24},{16,0},{24,8},{1,17},{9,25},{17,1},{25,9},{2,18},{10... | collective-permute-start | bytes 393224 | tf_op jit(solution)/shard_map/ppermute | solution.py:35
  22.2 1.5 %collective-permute-start.4 = (f32[4,64,128]{2,1,0:T(8,128)S(1)}, f32[4,64,128]{2,1,0:T(8,128)S(1)}, u32[]{:S(2)}, u32[]{:S(2)}) collective-permute-start(f32[4,64,128]{2,1,0:T(8,128)S(1)} %pad_maximum_fusion.refs_3_), channel_id=1, source_target_pairs={{0,8},{8,0},{16,24},{24,16},{1,9},{9,1},{17,25},{25,17},{2,10},{10... | collective-permute-start | bytes 393224 | tf_op jit(solution)/shard_map/ppermute | solution.py:35
  23.7 2.5 %collective-permute-done.6.refs_6_ = f32[4,64,128]{2,1,0:T(8,128)S(1)} collective-permute-done((f32[4,64,128]{2,1,0:T(8,128)S(1)}, f32[4,64,128]{2,1,0:T(8,128)S(1)}, u32[]{:S(2)}, u32[]{:S(2)}) %collective-permute-start.6) | collective-permute-done | bytes 131104 | tf_op jit(solution)/shard_map/ppermute | solution.py:35
  29.2 16.8 %shard_map.104 = (f32[1544,128]{1,0:T(8,128)S(1)}, f32[1544,128]{1,0:T(8,128)S(1)}) custom-call(s32[3]{0:T(128)S(1)} %pad_add_fusion.spot_ref.refs_0_, s32[8]{0:T(128)S(1)} %bitcast.28, s32[8]{0:T(128)S(1)} %bitcast.29, f32[4,64,128]{2,1,0:T(8,128)S(1)} %pad_maximum_fusion.refs_3_, f32[4,64,128]{2,1,0:T(8,128)S(1)} %collective-permute-done.4.refs_4_, ...), custom_call_target="tpu_custom_call" | custom-call | flops 4294967296 | bytes 4194304 | tf_op jit(solution)/shard_map/pallas_call | solution.py:247
  46.2 2.1 %collective-permute-done.11.refs_2_ = f32[1544,128]{1,0:T(8,128)S(1)} collective-permute-done((f32[1544,128]{1,0:T(8,128)S(1)}, f32[1544,128]{1,0:T(8,128)S(1)}, u32[]{:S(2)}, u32[]{:S(2)}) %collective-permute-start.11) | collective-permute-done | bytes 790560 | tf_op jit(solution)/shard_map/ppermute | solution.py:35
  49.0 1.6 %collective-permute-start.12 = (f32[392,128]{1,0:T(8,128)S(1)}, f32[392,128]{1,0:T(8,128)S(1)}, u32[]{:S(2)}, u32[]{:S(2)}) collective-permute-start(f32[392,128]{1,0:T(8,128)S(1)} %get-tuple-element.23), channel_id=1, source_target_pairs={{0,8},{8,0},{16,24},{24,16},{1,9},{9,1},{17,25},{25,17},{2,10},{10... | collective-permute-start | bytes 602120 | tf_op jit(solution)/shard_map/ppermute | solution.py:35
  50.7 1.8 %collective-permute-start.14 = (f32[392,128]{1,0:T(8,128)S(1)}, f32[392,128]{1,0:T(8,128)S(1)}, u32[]{:S(2)}, u32[]{:S(2)}) collective-permute-start(f32[392,128]{1,0:T(8,128)S(1)} %get-tuple-element.25), channel_id=1, source_target_pairs={{0,24},{8,16},{16,8},{24,0},{1,25},{9,17},{17,9},{25,1},{2,26},{10... | collective-permute-start | bytes 602120 | tf_op jit(solution)/shard_map/ppermute | solution.py:35
  52.5 4.4 %collective-permute-done.12 = f32[392,128]{1,0:T(8,128)S(1)} collective-permute-done((f32[392,128]{1,0:T(8,128)S(1)}, f32[392,128]{1,0:T(8,128)S(1)}, u32[]{:S(2)}, u32[]{:S(2)}) %collective-permute-start.12) | collective-permute-done | bytes 200736 | tf_op jit(solution)/shard_map/ppermute | solution.py:35
  56.9 4.7 %collective-permute-done.13 = f32[392,128]{1,0:T(8,128)S(1)} collective-permute-done((f32[392,128]{1,0:T(8,128)S(1)}, f32[392,128]{1,0:T(8,128)S(1)}, u32[]{:S(2)}, u32[]{:S(2)}) %collective-permute-start.13) | collective-permute-done | bytes 200736 | tf_op jit(solution)/shard_map/ppermute | solution.py:35
  61.7 3.5 %collective-permute-start.15 = (f32[128,128]{1,0:T(8,128)S(1)}, f32[128,128]{1,0:T(8,128)S(1)}, u32[]{:S(2)}, u32[]{:S(2)}) collective-permute-start(f32[128,128]{1,0:T(8,128)S(1)} %slice.32), channel_id=1, source_target_pairs={{0,2},{2,4},{4,6},{8,10},{10,12},{12,14},{18,16},{20,18},{22,20},{... | collective-permute-start | bytes 196616 | tf_op jit(solution)/shard_map/ppermute | solution.py:353
  65.2 1.9 %collective-permute-done.15 = f32[128,128]{1,0:T(8,128)S(1)} collective-permute-done((f32[128,128]{1,0:T(8,128)S(1)}, f32[128,128]{1,0:T(8,128)S(1)}, u32[]{:S(2)}, u32[]{:S(2)}) %collective-permute-start.15) | collective-permute-done | bytes 65568 | tf_op jit(solution)/shard_map/ppermute | solution.py:353
  67.1 3.4 %collective-permute-start.20 = (f32[144,128]{1,0:T(8,128)S(1)}, f32[144,128]{1,0:T(8,128)S(1)}, u32[]{:S(2)}, u32[]{:S(2)}) collective-permute-start(f32[144,128]{1,0:T(8,128)S(1)} %pad_maximum_fusion.1), channel_id=1, source_target_pairs={{0,4},{2,6},{4,0},{6,2},{1,5},{3,7},{5,1},{7,3},{8,12},{10,14},{12... | collective-permute-start | bytes 221192 | tf_op jit(solution)/shard_map/ppermute | solution.py:35
  70.5 1.3 %collective-permute-start.21 = (f32[144,128]{1,0:T(8,128)S(1)}, f32[144,128]{1,0:T(8,128)S(1)}, u32[]{:S(2)}, u32[]{:S(2)}) collective-permute-start(f32[144,128]{1,0:T(8,128)S(1)} %pad_maximum_fusion.1), channel_id=1, source_target_pairs={{0,6},{2,4},{4,2},{6,0},{1,7},{3,5},{5,3},{7,1},{8,14},{10,12},{12... | collective-permute-start | bytes 221192 | tf_op jit(solution)/shard_map/ppermute | solution.py:35
  71.9 2.1 %collective-permute-done.20 = f32[144,128]{1,0:T(8,128)S(1)} collective-permute-done((f32[144,128]{1,0:T(8,128)S(1)}, f32[144,128]{1,0:T(8,128)S(1)}, u32[]{:S(2)}, u32[]{:S(2)}) %collective-permute-start.20) | collective-permute-done | bytes 73760 | tf_op jit(solution)/shard_map/ppermute | solution.py:35
  74.0 2.8 %collective-permute-done.21 = f32[144,128]{1,0:T(8,128)S(1)} collective-permute-done((f32[144,128]{1,0:T(8,128)S(1)}, f32[144,128]{1,0:T(8,128)S(1)}, u32[]{:S(2)}, u32[]{:S(2)}) %collective-permute-start.21) | collective-permute-done | bytes 73760 | tf_op jit(solution)/shard_map/ppermute | solution.py:35
  77.0 1.2 %collective-permute-start.24 = (f32[144,128]{1,0:T(8,128)S(1)}, f32[144,128]{1,0:T(8,128)S(1)}, u32[]{:S(2)}, u32[]{:S(2)}) collective-permute-start(f32[144,128]{1,0:T(8,128)S(1)} %add_add_fusion.1.refs_5_), channel_id=1, source_target_pairs={{0,24},{8,16},{16,8},{24,0},{1,25},{9,17},{17,9},{25,1},{2,26},{10... | collective-permute-start | bytes 221192 | tf_op jit(solution)/shard_map/ppermute | solution.py:35
  78.3 1.0 %collective-permute-start.23 = (f32[144,128]{1,0:T(8,128)S(1)}, f32[144,128]{1,0:T(8,128)S(1)}, u32[]{:S(2)}, u32[]{:S(2)}) collective-permute-start(f32[144,128]{1,0:T(8,128)S(1)} %add_add_fusion.1.refs_5_), channel_id=1, source_target_pairs={{0,16},{8,24},{16,0},{24,8},{1,17},{9,25},{17,1},{25,9},{2,18},{10... | collective-permute-start | bytes 221192 | tf_op jit(solution)/shard_map/ppermute | solution.py:35
  79.3 1.3 %collective-permute-start.22 = (f32[144,128]{1,0:T(8,128)S(1)}, f32[144,128]{1,0:T(8,128)S(1)}, u32[]{:S(2)}, u32[]{:S(2)}) collective-permute-start(f32[144,128]{1,0:T(8,128)S(1)} %add_add_fusion.1.refs_5_), channel_id=1, source_target_pairs={{0,8},{8,0},{16,24},{24,16},{1,9},{9,1},{17,25},{25,17},{2,10},{10... | collective-permute-start | bytes 221192 | tf_op jit(solution)/shard_map/ppermute | solution.py:35
  80.6 1.2 %collective-permute-start.18 = (f32[128,128]{1,0:T(8,128)S(1)}, f32[128,128]{1,0:T(8,128)S(1)}, u32[]{:S(2)}, u32[]{:S(2)}) collective-permute-start(f32[128,128]{1,0:T(8,128)S(1)} %pad_maximum_fusion.3.refs_1_), channel_id=1, source_target_pairs={{0,24},{8,16},{16,8},{24,0},{1,25},{9,17},{17,9},{25,1},{2,26},{10... | collective-permute-start | bytes 196616 | tf_op jit(solution)/shard_map/ppermute | solution.py:35
  81.8 1.0 %collective-permute-start.17 = (f32[128,128]{1,0:T(8,128)S(1)}, f32[128,128]{1,0:T(8,128)S(1)}, u32[]{:S(2)}, u32[]{:S(2)}) collective-permute-start(f32[128,128]{1,0:T(8,128)S(1)} %pad_maximum_fusion.3.refs_1_), channel_id=1, source_target_pairs={{0,16},{8,24},{16,0},{24,8},{1,17},{9,25},{17,1},{25,9},{2,18},{10... | collective-permute-start | bytes 196616 | tf_op jit(solution)/shard_map/ppermute | solution.py:35
  82.8 3.0 %collective-permute-done.18.refs_4_ = f32[128,128]{1,0:T(8,128)S(1)} collective-permute-done((f32[128,128]{1,0:T(8,128)S(1)}, f32[128,128]{1,0:T(8,128)S(1)}, u32[]{:S(2)}, u32[]{:S(2)}) %collective-permute-start.18) | collective-permute-done | bytes 65568 | tf_op jit(solution)/shard_map/ppermute | solution.py:35
  87.6 3.5 %collective-permute-done.16.refs_2_ = f32[128,128]{1,0:T(8,128)S(1)} collective-permute-done((f32[128,128]{1,0:T(8,128)S(1)}, f32[128,128]{1,0:T(8,128)S(1)}, u32[]{:S(2)}, u32[]{:S(2)}) %collective-permute-start.16) | collective-permute-done | bytes 65568 | tf_op jit(solution)/shard_map/ppermute | solution.py:35
  91.1 1.5 %shard_map.106 = (f32[2,256,128]{2,1,0:T(8,128)}, f32[2,256,256]{2,1,0:T(8,128)}, f32[1,1]{1,0:T(1,128)}) custom-call(s32[3]{0:T(128)S(1)} %pad_add_fusion.spot_ref.refs_0_, f32[128,128]{1,0:T(8,128)S(1)} %pad_maximum_fusion.3.refs_1_, f32[128,128]{1,0:T(8,128)S(1)} %collective-permute-done.16.refs_2_, f32[128,128]{1,0:T(8,128)S(1)} %collective-permute-done.17.refs_3_, ...), custom_call_target="tpu_custom_call" | custom-call | bytes 851968 | tf_op jit(solution)/shard_map/pallas_call | solution.py:247
  (62 shorter events, 7.5 us)
Async XLA Ops:
  3.2 25.4 %copy-start.2 = (bf16[1,1,8,256,256]{4,3,2,1,0:T(8,128)(2,1)S(1)}, bf16[1,1,8,256,256]{4,3,2,1,0:T(8,128)(2,1)}, u32[]{:S(2)}) copy-start(bf16[1,1,8,256,256]{4,3,2,1,0:T(8,128)(2,1)} %param.11) | copy-start | bytes 3145732
  3.2 25.4 %copy-start.6 = (bf16[512,512]{1,0:T(8,128)(2,1)S(1)}, bf16[512,512]{1,0:T(8,128)(2,1)}, u32[]{:S(2)}) copy-start(bf16[512,512]{1,0:T(8,128)(2,1)} %constant.27.clone.refs_18_) | copy-start | bytes 1572868
  3.2 25.4 %copy-start.7 = (bf16[512,512]{1,0:T(8,128)(2,1)S(1)}, bf16[512,512]{1,0:T(8,128)(2,1)}, u32[]{:S(2)}) copy-start(bf16[512,512]{1,0:T(8,128)(2,1)} %constant.26.clone.refs_17_) | copy-start | bytes 1572868
  4.0 5.4 %collective-permute-start = (f32[2,64,128]{2,1,0:T(8,128)S(1)}, f32[2,64,128]{2,1,0:T(8,128)S(1)}, u32[]{:S(2)}, u32[]{:S(2)}) collective-permute-start(f32[2,64,128]{2,1,0:T(8,128)S(1)} %get-tuple-element.17), channel_id=1, source_target_pairs={{0,8},{8,0},{16,24},{24,16},{1,9},{9,1},{17,25},{25,17},{2,10},{10... | collective-permute-start | bytes 196616 | tf_op jit(solution)/shard_map/ppermute | solution.py:35
  7.0 4.3 %collective-permute-start.1 = (f32[2,64,128]{2,1,0:T(8,128)S(1)}, f32[2,64,128]{2,1,0:T(8,128)S(1)}, u32[]{:S(2)}, u32[]{:S(2)}) collective-permute-start(f32[2,64,128]{2,1,0:T(8,128)S(1)} %get-tuple-element.18), channel_id=1, source_target_pairs={{0,16},{8,24},{16,0},{24,8},{1,17},{9,25},{17,1},{25,9},{2,18},{10... | collective-permute-start | bytes 196616 | tf_op jit(solution)/shard_map/ppermute | solution.py:35
  8.6 5.2 %collective-permute-start.2 = (f32[2,64,128]{2,1,0:T(8,128)S(1)}, f32[2,64,128]{2,1,0:T(8,128)S(1)}, u32[]{:S(2)}, u32[]{:S(2)}) collective-permute-start(f32[2,64,128]{2,1,0:T(8,128)S(1)} %get-tuple-element.19), channel_id=1, source_target_pairs={{0,24},{8,16},{16,8},{24,0},{1,25},{9,17},{17,9},{25,1},{2,26},{10... | collective-permute-start | bytes 196616 | tf_op jit(solution)/shard_map/ppermute | solution.py:35
  13.9 6.2 %collective-permute-start.3 = (f32[2,64,128]{2,1,0:T(8,128)S(1)}, f32[2,64,128]{2,1,0:T(8,128)S(1)}, u32[]{:S(2)}, u32[]{:S(2)}) collective-permute-start(f32[2,64,128]{2,1,0:T(8,128)S(1)} %pad_maximum_fusion.2), channel_id=1, source_target_pairs={{2,0},{4,2},{6,4},{10,8},{12,10},{14,12},{16,18},{18,20},{20,22},{... | collective-permute-start | bytes 196616 | tf_op jit(solution)/shard_map/ppermute | solution.py:291
  20.1 6.0 %collective-permute-start.6 = (f32[4,64,128]{2,1,0:T(8,128)S(1)}, f32[4,64,128]{2,1,0:T(8,128)S(1)}, u32[]{:S(2)}, u32[]{:S(2)}) collective-permute-start(f32[4,64,128]{2,1,0:T(8,128)S(1)} %pad_maximum_fusion.refs_3_), channel_id=1, source_target_pairs={{0,24},{8,16},{16,8},{24,0},{1,25},{9,17},{17,9},{25,1},{2,26},{10... | collective-permute-start | bytes 393224 | tf_op jit(solution)/shard_map/ppermute | solution.py:35
  20.2 6.4 %collective-permute-start.5 = (f32[4,64,128]{2,1,0:T(8,128)S(1)}, f32[4,64,128]{2,1,0:T(8,128)S(1)}, u32[]{:S(2)}, u32[]{:S(2)}) collective-permute-start(f32[4,64,128]{2,1,0:T(8,128)S(1)} %pad_maximum_fusion.refs_3_), channel_id=1, source_target_pairs={{0,16},{8,24},{16,0},{24,8},{1,17},{9,25},{17,1},{25,9},{2,18},{10... | collective-permute-start | bytes 393224 | tf_op jit(solution)/shard_map/ppermute | solution.py:35
  22.2 5.0 %collective-permute-start.4 = (f32[4,64,128]{2,1,0:T(8,128)S(1)}, f32[4,64,128]{2,1,0:T(8,128)S(1)}, u32[]{:S(2)}, u32[]{:S(2)}) collective-permute-start(f32[4,64,128]{2,1,0:T(8,128)S(1)} %pad_maximum_fusion.refs_3_), channel_id=1, source_target_pairs={{0,8},{8,0},{16,24},{24,16},{1,9},{9,1},{17,25},{25,17},{2,10},{10... | collective-permute-start | bytes 393224 | tf_op jit(solution)/shard_map/ppermute | solution.py:35
  23.7 3.5 %collective-permute-start.7 = (f32[4,64,128]{2,1,0:T(8,128)S(1)}, f32[4,64,128]{2,1,0:T(8,128)S(1)}, u32[]{:S(2)}, u32[]{:S(2)}) collective-permute-start(f32[4,64,128]{2,1,0:T(8,128)S(1)} %pad_maximum_fusion.refs_3_), channel_id=1, source_target_pairs={{0,1},{1,0},{2,3},{3,2},{4,5},{5,4},{6,7},{7,6},{8,9},{9,8},{10,11... | collective-permute-start | bytes 393224 | tf_op jit(solution)/shard_map/ppermute | solution.py:35
  26.2 1.3 %collective-permute-start.10 = (f32[4,64,128]{2,1,0:T(8,128)S(1)}, f32[4,64,128]{2,1,0:T(8,128)S(1)}, u32[]{:S(2)}, u32[]{:S(2)}) collective-permute-start(f32[4,64,128]{2,1,0:T(8,128)S(1)} %collective-permute-done.6.refs_6_), channel_id=1, source_target_pairs={{0,1},{1,0},{2,3},{3,2},{4,5},{5,4},{6,7},{7,6},{8,9},{9,8},{10,11... | collective-permute-start | bytes 393224 | tf_op jit(solution)/shard_map/ppermute | solution.py:35
  26.7 1.3 %collective-permute-start.9 = (f32[4,64,128]{2,1,0:T(8,128)S(1)}, f32[4,64,128]{2,1,0:T(8,128)S(1)}, u32[]{:S(2)}, u32[]{:S(2)}) collective-permute-start(f32[4,64,128]{2,1,0:T(8,128)S(1)} %collective-permute-done.5.refs_5_), channel_id=1, source_target_pairs={{0,1},{1,0},{2,3},{3,2},{4,5},{5,4},{6,7},{7,6},{8,9},{9,8},{10,11... | collective-permute-start | bytes 393224 | tf_op jit(solution)/shard_map/ppermute | solution.py:35
  27.2 1.3 %collective-permute-start.8 = (f32[4,64,128]{2,1,0:T(8,128)S(1)}, f32[4,64,128]{2,1,0:T(8,128)S(1)}, u32[]{:S(2)}, u32[]{:S(2)}) collective-permute-start(f32[4,64,128]{2,1,0:T(8,128)S(1)} %collective-permute-done.4.refs_4_), channel_id=1, source_target_pairs={{0,1},{1,0},{2,3},{3,2},{4,5},{5,4},{6,7},{7,6},{8,9},{9,8},{10,11... | collective-permute-start | bytes 393224 | tf_op jit(solution)/shard_map/ppermute | solution.py:35
  46.0 2.4 %collective-permute-start.11 = (f32[1544,128]{1,0:T(8,128)S(1)}, f32[1544,128]{1,0:T(8,128)S(1)}, u32[]{:S(2)}, u32[]{:S(2)}) collective-permute-start(f32[1544,128]{1,0:T(8,128)S(1)} %get-tuple-element.21), channel_id=1, source_target_pairs={{0,1},{1,0},{2,3},{3,2},{4,5},{5,4},{6,7},{7,6},{8,9},{9,8},{10,11... | collective-permute-start | bytes 2371592 | tf_op jit(solution)/shard_map/ppermute | solution.py:35
  49.0 7.9 %collective-permute-start.12 = (f32[392,128]{1,0:T(8,128)S(1)}, f32[392,128]{1,0:T(8,128)S(1)}, u32[]{:S(2)}, u32[]{:S(2)}) collective-permute-start(f32[392,128]{1,0:T(8,128)S(1)} %get-tuple-element.23), channel_id=1, source_target_pairs={{0,8},{8,0},{16,24},{24,16},{1,9},{9,1},{17,25},{25,17},{2,10},{10... | collective-permute-start | bytes 602120 | tf_op jit(solution)/shard_map/ppermute | solution.py:35
  50.5 11.1 %collective-permute-start.13 = (f32[392,128]{1,0:T(8,128)S(1)}, f32[392,128]{1,0:T(8,128)S(1)}, u32[]{:S(2)}, u32[]{:S(2)}) collective-permute-start(f32[392,128]{1,0:T(8,128)S(1)} %get-tuple-element.24), channel_id=1, source_target_pairs={{0,16},{8,24},{16,0},{24,8},{1,17},{9,25},{17,1},{25,9},{2,18},{10... | collective-permute-start | bytes 602120 | tf_op jit(solution)/shard_map/ppermute | solution.py:35
  50.7 10.9 %collective-permute-start.14 = (f32[392,128]{1,0:T(8,128)S(1)}, f32[392,128]{1,0:T(8,128)S(1)}, u32[]{:S(2)}, u32[]{:S(2)}) collective-permute-start(f32[392,128]{1,0:T(8,128)S(1)} %get-tuple-element.25), channel_id=1, source_target_pairs={{0,24},{8,16},{16,8},{24,0},{1,25},{9,17},{17,9},{25,1},{2,26},{10... | collective-permute-start | bytes 602120 | tf_op jit(solution)/shard_map/ppermute | solution.py:35
  61.7 5.4 %collective-permute-start.15 = (f32[128,128]{1,0:T(8,128)S(1)}, f32[128,128]{1,0:T(8,128)S(1)}, u32[]{:S(2)}, u32[]{:S(2)}) collective-permute-start(f32[128,128]{1,0:T(8,128)S(1)} %slice.32), channel_id=1, source_target_pairs={{0,2},{2,4},{4,6},{8,10},{10,12},{12,14},{18,16},{20,18},{22,20},{... | collective-permute-start | bytes 196616 | tf_op jit(solution)/shard_map/ppermute | solution.py:353
  67.1 6.9 %collective-permute-start.20 = (f32[144,128]{1,0:T(8,128)S(1)}, f32[144,128]{1,0:T(8,128)S(1)}, u32[]{:S(2)}, u32[]{:S(2)}) collective-permute-start(f32[144,128]{1,0:T(8,128)S(1)} %pad_maximum_fusion.1), channel_id=1, source_target_pairs={{0,4},{2,6},{4,0},{6,2},{1,5},{3,7},{5,1},{7,3},{8,12},{10,14},{12... | collective-permute-start | bytes 221192 | tf_op jit(solution)/shard_map/ppermute | solution.py:35
  70.5 6.3 %collective-permute-start.21 = (f32[144,128]{1,0:T(8,128)S(1)}, f32[144,128]{1,0:T(8,128)S(1)}, u32[]{:S(2)}, u32[]{:S(2)}) collective-permute-start(f32[144,128]{1,0:T(8,128)S(1)} %pad_maximum_fusion.1), channel_id=1, source_target_pairs={{0,6},{2,4},{4,2},{6,0},{1,7},{3,5},{5,3},{7,1},{8,14},{10,12},{12... | collective-permute-start | bytes 221192 | tf_op jit(solution)/shard_map/ppermute | solution.py:35
  71.9 5.1 %collective-permute-start.19 = (f32[144,128]{1,0:T(8,128)S(1)}, f32[144,128]{1,0:T(8,128)S(1)}, u32[]{:S(2)}, u32[]{:S(2)}) collective-permute-start(f32[144,128]{1,0:T(8,128)S(1)} %pad_maximum_fusion.1), channel_id=1, source_target_pairs={{0,2},{2,0},{4,6},{6,4},{1,3},{3,1},{5,7},{7,5},{8,10},{10,8},{12,... | collective-permute-start | bytes 221192 | tf_op jit(solution)/shard_map/ppermute | solution.py:35
  77.0 8.8 %collective-permute-start.24 = (f32[144,128]{1,0:T(8,128)S(1)}, f32[144,128]{1,0:T(8,128)S(1)}, u32[]{:S(2)}, u32[]{:S(2)}) collective-permute-start(f32[144,128]{1,0:T(8,128)S(1)} %add_add_fusion.1.refs_5_), channel_id=1, source_target_pairs={{0,24},{8,16},{16,8},{24,0},{1,25},{9,17},{17,9},{25,1},{2,26},{10... | collective-permute-start | bytes 221192 | tf_op jit(solution)/shard_map/ppermute | solution.py:35
  78.3 8.0 %collective-permute-start.23 = (f32[144,128]{1,0:T(8,128)S(1)}, f32[144,128]{1,0:T(8,128)S(1)}, u32[]{:S(2)}, u32[]{:S(2)}) collective-permute-start(f32[144,128]{1,0:T(8,128)S(1)} %add_add_fusion.1.refs_5_), channel_id=1, source_target_pairs={{0,16},{8,24},{16,0},{24,8},{1,17},{9,25},{17,1},{25,9},{2,18},{10... | collective-permute-start | bytes 221192 | tf_op jit(solution)/shard_map/ppermute | solution.py:35
  79.3 7.1 %collective-permute-start.22 = (f32[144,128]{1,0:T(8,128)S(1)}, f32[144,128]{1,0:T(8,128)S(1)}, u32[]{:S(2)}, u32[]{:S(2)}) collective-permute-start(f32[144,128]{1,0:T(8,128)S(1)} %add_add_fusion.1.refs_5_), channel_id=1, source_target_pairs={{0,8},{8,0},{16,24},{24,16},{1,9},{9,1},{17,25},{25,17},{2,10},{10... | collective-permute-start | bytes 221192 | tf_op jit(solution)/shard_map/ppermute | solution.py:35
  80.6 5.2 %collective-permute-start.18 = (f32[128,128]{1,0:T(8,128)S(1)}, f32[128,128]{1,0:T(8,128)S(1)}, u32[]{:S(2)}, u32[]{:S(2)}) collective-permute-start(f32[128,128]{1,0:T(8,128)S(1)} %pad_maximum_fusion.3.refs_1_), channel_id=1, source_target_pairs={{0,24},{8,16},{16,8},{24,0},{1,25},{9,17},{17,9},{25,1},{2,26},{10... | collective-permute-start | bytes 196616 | tf_op jit(solution)/shard_map/ppermute | solution.py:35
  81.8 5.1 %collective-permute-start.17 = (f32[128,128]{1,0:T(8,128)S(1)}, f32[128,128]{1,0:T(8,128)S(1)}, u32[]{:S(2)}, u32[]{:S(2)}) collective-permute-start(f32[128,128]{1,0:T(8,128)S(1)} %pad_maximum_fusion.3.refs_1_), channel_id=1, source_target_pairs={{0,16},{8,24},{16,0},{24,8},{1,17},{9,25},{17,1},{25,9},{2,18},{10... | collective-permute-start | bytes 196616 | tf_op jit(solution)/shard_map/ppermute | solution.py:35
  85.8 5.3 %collective-permute-start.25 = (f32[144,128]{1,0:T(8,128)S(1)}, f32[144,128]{1,0:T(8,128)S(1)}, u32[]{:S(2)}, u32[]{:S(2)}) collective-permute-start(f32[144,128]{1,0:T(8,128)S(1)} %add_add_fusion.1.refs_5_), channel_id=1, source_target_pairs={{0,1},{1,0},{2,3},{3,2},{4,5},{5,4},{6,7},{7,6},{8,9},{9,8},{10,11... | collective-permute-start | bytes 221192 | tf_op jit(solution)/shard_map/ppermute | solution.py:35
  85.8 5.3 %collective-permute-start.28 = (f32[144,128]{1,0:T(8,128)S(1)}, f32[144,128]{1,0:T(8,128)S(1)}, u32[]{:S(2)}, u32[]{:S(2)}) collective-permute-start(f32[144,128]{1,0:T(8,128)S(1)} %collective-permute-done.24.refs_8_), channel_id=1, source_target_pairs={{0,1},{1,0},{2,3},{3,2},{4,5},{5,4},{6,7},{7,6},{8,9},{9,8},{10,11... | collective-permute-start | bytes 221192 | tf_op jit(solution)/shard_map/ppermute | solution.py:35
  86.3 4.8 %collective-permute-start.27 = (f32[144,128]{1,0:T(8,128)S(1)}, f32[144,128]{1,0:T(8,128)S(1)}, u32[]{:S(2)}, u32[]{:S(2)}) collective-permute-start(f32[144,128]{1,0:T(8,128)S(1)} %collective-permute-done.23.refs_7_), channel_id=1, source_target_pairs={{0,1},{1,0},{2,3},{3,2},{4,5},{5,4},{6,7},{7,6},{8,9},{9,8},{10,11... | collective-permute-start | bytes 221192 | tf_op jit(solution)/shard_map/ppermute | solution.py:35
  86.4 4.7 %collective-permute-start.26 = (f32[144,128]{1,0:T(8,128)S(1)}, f32[144,128]{1,0:T(8,128)S(1)}, u32[]{:S(2)}, u32[]{:S(2)}) collective-permute-start(f32[144,128]{1,0:T(8,128)S(1)} %collective-permute-done.22.refs_6_), channel_id=1, source_target_pairs={{0,1},{1,0},{2,3},{3,2},{4,5},{5,4},{6,7},{7,6},{8,9},{9,8},{10,11... | collective-permute-start | bytes 221192 | tf_op jit(solution)/shard_map/ppermute | solution.py:35
  86.9 4.3 %collective-permute-start.16 = (f32[128,128]{1,0:T(8,128)S(1)}, f32[128,128]{1,0:T(8,128)S(1)}, u32[]{:S(2)}, u32[]{:S(2)}) collective-permute-start(f32[128,128]{1,0:T(8,128)S(1)} %pad_maximum_fusion.3.refs_1_), channel_id=1, source_target_pairs={{0,8},{8,0},{16,24},{24,16},{1,9},{9,1},{17,25},{25,17},{2,10},{10... | collective-permute-start | bytes 196616 | tf_op jit(solution)/shard_map/ppermute | solution.py:35
  (5 other events, 28.3 us)
